TPU v7x, 32 devices: a whole 2x2x4 slice. The times are simulated.
32 devices in a mesh: dp: 8 (over z, x), expert: 4 (over y, core).
Axes of the slice: x: 2, y: 2, z: 4, core: 2. Of those that a mesh axis runs over, the one named last changes fastest.
Arguments:
- tokens: bfloat16 [4096, 2048], P(('dp', 'expert')), may hold values from -6 to 6
- out_grad: bfloat16 [4096, 2048], P(('dp', 'expert')), may hold values from -3 to 3
- z_weight: float32 [4096], P(('dp', 'expert')), may hold values from 0.1 to 1
- router_weight: bfloat16 [2048, 128], replicated, may hold values from -0.125 to 0.125
- expert_ids: int32 [4096, 4], P(('dp', 'expert')), may hold values from 0 to 127, as said below
- gate_up_weight: bfloat16 [4, 2048, 3072], P('expert'), may hold values from -0.125 to 0.125
- down_weight: bfloat16 [4, 1536, 2048], P('expert'), may hold values from -0.15625 to 0.15625
Outputs:
- token_grad: bfloat16 [4096, 2048], P(('dp', 'expert'))
- router_grad: float32 [2048, 128], replicated
- gate_up_grad: bfloat16 [4, 2048, 3072], P('expert', 'dp')
- down_grad: bfloat16 [4, 1536, 2048], P('expert', 'dp')
Inputs may be any that keep to these rules, and one draw needn't show every extreme that they name: `expert_ids`: each row names 4 different experts. Experts 0 to 3 are the ones in flight. The 128 rows of one device name any one expert in flight at most 64 times; in every data group some expert in flight is named exactly 64 times by the rows of each device of the group.
All inputs are finite; a program needn't handle non-finite values.
Results may differ from a plain program's by a relative error of at most 0.019.
Values may be sent and summed in bfloat16 or wider, within the bound.
A program may use at most 192 MiB of HBM per device.

v0:
```python
import jax
import jax.numpy as jnp
from jax import lax
from jax.sharding import PartitionSpec as P


def expert_rows(rows_in, rows_grad, w_gateup, w_down, acc_gateup, acc_down):
    hidden_units = w_down.shape[0]
    pre_act = jnp.dot(rows_in, w_gateup, preferred_element_type=jnp.float32)
    gate_pre = pre_act[:, :hidden_units]
    up_pre = pre_act[:, hidden_units:]
    activated = jax.nn.silu(gate_pre)
    hidden = (activated * up_pre).astype(jnp.bfloat16)
    expert_out = jnp.dot(hidden, w_down, preferred_element_type=jnp.float32).astype(jnp.bfloat16)
    hidden_grad = lax.dot_general(
        rows_grad, w_down, (((1,), (1,)), ((), ())), preferred_element_type=jnp.float32
    )
    acc_down = lax.dot_general(
        hidden, rows_grad, (((0,), (0,)), ((), ())), preferred_element_type=jnp.float32
    )
    sigmoid_gate = jax.nn.sigmoid(gate_pre)
    gate_grad = hidden_grad * up_pre * sigmoid_gate * (1.0 + gate_pre * (1.0 - sigmoid_gate))
    up_grad = hidden_grad * activated
    pre_grad = jnp.concatenate([gate_grad, up_grad], axis=1).astype(jnp.bfloat16)
    acc_gateup = lax.dot_general(
        rows_in, pre_grad, (((0,), (0,)), ((), ())), preferred_element_type=jnp.float32
    )
    input_grad = lax.dot_general(
        pre_grad, w_gateup, (((1,), (1,)), ((), ())), preferred_element_type=jnp.float32
    ).astype(jnp.bfloat16)
    return (acc_gateup, acc_down, expert_out, input_grad)


def split_pair(values):
    upper = values.astype(jnp.bfloat16)
    lower = (values - upper.astype(jnp.float32)).astype(jnp.bfloat16)
    return jnp.stack([upper, lower], axis=-1)


def join_pair(pair):
    return pair[..., 0].astype(jnp.float32) + pair[..., 1].astype(jnp.float32)


def per_device(tokens, out_grad, z_weight, router_weight, expert_ids, gate_up_weight, down_weight):
    tok_count, width = tokens.shape
    top_count = expert_ids.shape[1]
    routed = router_weight.shape[1]
    flight = lax.axis_size("expert")
    capacity = tok_count // 2
    w_gateup = gate_up_weight[0]
    w_down = down_weight[0]
    hidden_units = w_down.shape[0]
    logits = jnp.dot(tokens, router_weight, preferred_element_type=jnp.float32)
    choose = expert_ids[:, :, None] == jnp.arange(routed, dtype=jnp.int32)[None, None, :]
    selected = jnp.sum(jnp.where(choose, logits[:, None, :], 0.0), axis=2)
    sel_exp = jnp.exp(selected)
    probs = sel_exp / jnp.sum(sel_exp, axis=1, keepdims=True)
    log_total = jnp.log(jnp.sum(jnp.exp(logits), axis=1))
    flat_ids = expert_ids.reshape(-1)
    slot_count = tok_count * top_count
    member = (flat_ids[:, None] == jnp.arange(flight, dtype=jnp.int32)[None, :]).astype(jnp.int32)
    ranks = jnp.sum((jnp.cumsum(member, axis=0) - 1) * member, axis=1)
    in_flight = flat_ids < flight
    position = jnp.where(in_flight, flat_ids * capacity + ranks, flight * capacity)
    source_slot = (
        jnp.zeros((flight * capacity,), jnp.int32)
        .at[position]
        .set(jnp.arange(slot_count, dtype=jnp.int32), mode="drop")
    )
    filled = jnp.zeros((flight * capacity,), jnp.bool_).at[position].set(True, mode="drop")
    source_tok = source_slot // top_count
    send_in = jnp.where(filled[:, None], tokens[source_tok], 0)
    slot_prob = jnp.where(filled, probs.reshape(-1)[source_slot], 0.0)
    counts = jnp.sum(member, axis=0)
    count_msg = jnp.stack([counts // 128, counts % 128], axis=1).astype(jnp.bfloat16)
    send_raw = jnp.where(filled[:, None], out_grad[source_tok], 0)
    prob_pair = split_pair(slot_prob)
    recv_in, recv_raw, recv_prob, recv_counts = (
        lax.all_to_all(
            send_in.reshape(flight, capacity, width),
            "expert",
            split_axis=0,
            concat_axis=0,
            tiled=True,
        ),
        lax.all_to_all(
            send_raw.reshape(flight, capacity, width),
            "expert",
            split_axis=0,
            concat_axis=0,
            tiled=True,
        ),
        lax.all_to_all(
            prob_pair.reshape(flight, capacity, 2),
            "expert",
            split_axis=0,
            concat_axis=0,
            tiled=True,
        ),
        lax.all_to_all(count_msg, "expert", split_axis=0, concat_axis=0, tiled=True),
    )
    sources = recv_in.shape[0]
    total_rows = sources * capacity
    flat_in = recv_in.reshape(total_rows, width)
    flat_raw = recv_raw.reshape(total_rows, width)
    row_prob = join_pair(recv_prob.reshape(total_rows, 2))
    flat_grad = (row_prob[:, None] * flat_raw.astype(jnp.float32)).astype(jnp.bfloat16)
    acc_gateup, acc_down, produced, back_rows = expert_rows(
        flat_in,
        flat_grad,
        w_gateup,
        w_down,
        jnp.zeros((width, 2 * hidden_units), jnp.float32),
        jnp.zeros((hidden_units, width), jnp.float32),
    )
    slot_at = jnp.where(in_flight, position, 0)
    row_score = jnp.sum(flat_raw.astype(jnp.float32) * produced.astype(jnp.float32), axis=1)
    score_pair = split_pair(row_score)
    home_dx, home_pair = (
        lax.all_to_all(
            back_rows.reshape(sources, capacity, width),
            "expert",
            split_axis=0,
            concat_axis=0,
            tiled=True,
        ),
        lax.all_to_all(
            score_pair.reshape(sources, capacity, 2),
            "expert",
            split_axis=0,
            concat_axis=0,
            tiled=True,
        ),
    )
    flat_dx = home_dx.reshape(flight * capacity, width)
    flat_score = join_pair(home_pair.reshape(flight * capacity, 2))
    scores = jnp.where(in_flight, flat_score[slot_at], 0.0).reshape(tok_count, top_count)
    slot_dx = jnp.where(in_flight[:, None], flat_dx[slot_at], 0).reshape(
        tok_count, top_count, width
    )
    mean_score = jnp.sum(probs * scores, axis=1, keepdims=True)
    sel_grad = probs * (scores - mean_score)
    z_grad = 2.0 * z_weight[:, None] * log_total[:, None] * jnp.exp(logits - log_total[:, None])
    logit_grad = (z_grad + jnp.sum(jnp.where(choose, sel_grad[:, :, None], 0.0), axis=1)).astype(
        jnp.bfloat16
    )
    token_grad = (
        jnp.sum(slot_dx.astype(jnp.float32), axis=1)
        + lax.dot_general(
            logit_grad, router_weight, (((1,), (1,)), ((), ())), preferred_element_type=jnp.float32
        )
    ).astype(jnp.bfloat16)
    router_part = lax.dot_general(
        tokens, logit_grad, (((0,), (0,)), ((), ())), preferred_element_type=jnp.float32
    )
    router_grad = lax.psum(router_part, ("dp", "expert"))
    part_gateup = acc_gateup.astype(jnp.bfloat16)
    part_down = acc_down.astype(jnp.bfloat16)
    gate_up_grad, down_grad = (
        lax.psum_scatter(part_gateup[None], "dp", scatter_dimension=1, tiled=True).astype(
            jnp.float32
        ),
        lax.psum_scatter(part_down[None], "dp", scatter_dimension=1, tiled=True).astype(
            jnp.float32
        ),
    )
    return (
        token_grad,
        router_grad,
        gate_up_grad.astype(jnp.bfloat16),
        down_grad.astype(jnp.bfloat16),
    )


def solution(mesh):
    return jax.shard_map(
        per_device,
        mesh=mesh,
        in_specs=(
            P(("dp", "expert"), None),
            P(("dp", "expert"), None),
            P(("dp", "expert")),
            P(),
            P(("dp", "expert"), None),
            P("expert", None, None),
            P("expert", None, None),
        ),
        out_specs=(
            P(("dp", "expert"), None),
            P(),
            P("expert", "dp", None),
            P("expert", "dp", None),
        ),
        check_vma=False,
    )
```

profile of v0, /device:TPU:0, one launch (start us, length us, event | category | flops | bytes accessed | tf_op | source)
XLA Modules:
  0.0 440.1 jit_solution(1820209398362379599)
XLA Ops:
  13.3 2.4 scatter_custom_fusion.1
  15.8 2.4 scatter_custom_fusion
  23.2 4.4 all-to-all-start.2
  29.0 13.1 %all-to-all-done.2 = bf16[4,64,2048]{2,1,0:T(8,128)(2,1)S(1)} async-done(((bf16[4,64,2048]{2,1,0:T(8,128)(2,1)}), bf16[4,64,2048]{2,1,0:T(8,128)(2,1)S(1)}, u32[]{:S(2)}, u32[]{:S(2)}) %all-to-all-start.2) | async-done | bytes 1048608 | tf_op jit(solution)/shard_map/all_to_all | solution.py:79
  42.0 3.5 all-to-all-start.1
  45.6 9.7 %fusion.2 = f32[256,3072]{1,0:T(8,128)} fusion(bf16[256,2048]{1,0:T(8,128)(2,1)S(1)} %bitcast.81, bf16[1,2048,3072]{2,1,0:T(8,128)(2,1)} %param.12), kind=kOutput, calls=%fused_computation.9 | convolution fusion | flops 3221225472 | bytes 16777216 | tf_op jit(solution)/shard_map/dot_general | solution.py:9
  55.2 2.3 multiply_convert_fusion.1
  57.6 2.4 all-to-all-done.1
  60.0 4.8 %fusion.24 = f32[256]{0:T(256)S(1)} fusion(bf16[256,1536]{1,0:T(8,128)(2,1)S(1)} %multiply_convert_fusion.1, bf16[1,1536,2048]{2,1,0:T(8,128)(2,1)} %param.13, bf16[256,2048]{1,0:T(8,128)(2,1)S(1)} %bitcast.80), kind=kOutput, calls=%fused_computation.35 | convolution fusion | flops 1613233920 | bytes 8127488 | tf_op jit(solution)/shard_map/dot_general | solution.py:14
  65.4 3.4 all-to-all-start.4
  69.4 3.0 all-to-all-done.4
  72.4 3.5 gather_fusion.4
  82.8 3.2 all-to-all-start
  91.2 4.4 %fusion.4 = bf16[1,1536,2048]{2,1,0:T(8,128)(2,1)} fusion(bf16[256,1536]{1,0:T(8,128)(2,1)S(1)} %multiply_convert_fusion.1, bf16[256,2048]{1,0:T(8,128)(2,1)S(1)} %fusion.22), kind=kOutput, calls=%fused_computation.13 | convolution fusion | flops 1613758464 | bytes 8126464 | tf_op jit(solution)/shard_map/dot_general | solution.py:18
  96.1 6.0 %multiply_convert_fusion.3 = (bf16[256,1536]{1,0:T(8,128)(2,1)S(1)}, bf16[256,1536]{1,0:T(8,128)(2,1)S(1)}) fusion(f32[256,3072]{1,0:T(8,128)} %fusion.2, bf16[256,2048]{1,0:T(8,128)(2,1)S(1)} %bitcast.85, bf16[1,1536,2048]{2,1,0:T(8,128)(2,1)} %param.13), kind=kOutput, calls=%fused_computation.32 | convolution fusion | flops 1615724544 | bytes 12058624 | tf_op jit(solution)/shard_map/dot_general | solution.py:15
  102.1 6.6 %convert_bitcast_fusion = bf16[1,2048,3072]{2,1,0:T(8,128)(2,1)} fusion(bf16[256,2048]{1,0:T(8,128)(2,1)S(1)} %bitcast.82, bf16[256,1536]{1,0:T(8,128)(2,1)S(1)} %get-tuple-element.31, bf16[256,1536]{1,0:T(8,128)(2,1)S(1)} %get-tuple-element.30), kind=kOutput, calls=%fused_computation.11 | convolution fusion | flops 3230662656 | bytes 15204352 | tf_op jit(solution)/shard_map/dot_general | solution.py:25
  108.7 9.0 %fusion.18 = bf16[256,2048]{1,0:T(8,128)(2,1)} fusion(bf16[1,2048,3072]{2,1,0:T(8,128)(2,1)} %param.12, bf16[256,1536]{1,0:T(8,128)(2,1)S(1)} %get-tuple-element.31, bf16[256,1536]{1,0:T(8,128)(2,1)S(1)} %get-tuple-element.30), kind=kOutput, calls=%fused_computation.22 | convolution fusion | flops 3224895488 | bytes 15204352 | tf_op jit(solution)/shard_map/dot_general | solution.py:28
  117.8 3.9 all-to-all-start.3
  121.7 229.6 %all-reduce.2.cloned.1.call-done = f32[2048,128]{0,1:T(8,128)} async-done(((f32[2048,128]{0,1:T(8,128)}), f32[2048,128]{0,1:T(8,128)}) %all-reduce.2.cloned.1.call-update) | async-done | bytes 1048592 | tf_op jit(solution)/shard_map/psum | solution.py:156
  351.2 2.6 copy.55
  353.8 2.5 gather_fusion.3
  356.3 2.2 gather.29
  358.6 5.6 %convert_reduce_fusion = f32[128,2048]{1,0:T(8,128)S(1)} fusion(bf16[128,4,2048]{2,1,0:T(4,128)(2,1)} %gather.29, pred[128,4]{1,0:T(8,128)(4,1)S(1)} %copy-done.6), kind=kLoop, calls=%fused_computation.18 | loop fusion | flops 2883584 | bytes 3146240 | tf_op jit(solution)/shard_map/reduce_sum | solution.py:148
  365.3 67.3 %reduce-scatter.3.cloned.1.call-done = bf16[1,256,3072]{2,1,0:T(8,128)(2,1)} async-done(((bf16[1,2048,3072]{2,1,0:T(8,128)(2,1)}), bf16[1,256,3072]{2,1,0:T(8,128)(2,1)}) %reduce-scatter.3.cloned.1.call-update) | async-done | bytes 1572880 | tf_op jit(solution)/shard_map/reduce_scatter | solution.py:160
  (97 shorter events, 26.4 us)
Async XLA Ops:
  8.0 10.9 %copy-start = (bf16[128,2048]{1,0:T(8,128)(2,1)S(1)}, bf16[128,2048]{1,0:T(8,128)(2,1)}, u32[]{:S(2)}) copy-start(bf16[128,2048]{1,0:T(8,128)(2,1)} %param.7) | copy-start | bytes 1572868
  10.6 0.6 copy-start.5
  18.2 0.7 copy-start.11
  18.9 1.4 copy-start.2
  23.2 4.4 %copy-start.3 = (bf16[2048,128]{1,0:T(8,128)(2,1)S(1)}, bf16[2048,128]{1,0:T(8,128)(2,1)}, u32[]{:S(2)}) copy-start(bf16[2048,128]{1,0:T(8,128)(2,1)} %param.10) | copy-start | bytes 1572868
  23.2 4.9 %copy-start.7 = (s32[128,4]{0,1:T(4,128)S(1)}, s32[128,4]{0,1:T(4,128)}, u32[]{:S(2)}) copy-start(s32[128,4]{0,1:T(4,128)} %param.11) | copy-start | bytes 6148
  23.2 5.1 %copy-start.12 = (f32[128]{0:T(128)S(1)}, f32[128]{0:T(128)}, u32[]{:S(2)}) copy-start(f32[128]{0:T(128)} %param.9) | copy-start | bytes 1540
  23.2 18.8 %all-to-all-start.2 = ((bf16[4,64,2048]{2,1,0:T(8,128)(2,1)}), bf16[4,64,2048]{2,1,0:T(8,128)(2,1)S(1)}, u32[]{:S(2)}, u32[]{:S(2)}) async-start(bf16[4,64,2048]{2,1,0:T(8,128)(2,1)} %get-tuple-element.38), calls=%async_computation.2 | async-start | bytes 2097152 | tf_op jit(solution)/shard_map/all_to_all | solution.py:79
  28.1 44.3 %copy-start.9 = (s32[1024]{0:T(1024)}, s32[1024]{0:T(1024)S(1)}, u32[]{:S(2)}) copy-start(s32[1024]{0:T(1024)S(1)} %pad_clamp_fusion) | copy-start | bytes 12292
  42.0 17.9 %all-to-all-start.1 = ((bf16[4,64,2048]{2,1,0:T(8,128)(2,1)}), bf16[4,64,2048]{2,1,0:T(8,128)(2,1)S(1)}, u32[]{:S(2)}, u32[]{:S(2)}) async-start(bf16[4,64,2048]{2,1,0:T(8,128)(2,1)} %get-tuple-element.39), calls=%async_computation.1 | async-start | bytes 2097152 | tf_op jit(solution)/shard_map/all_to_all | solution.py:86
  65.4 6.9 %all-to-all-start.4 = ((bf16[4,64,2]{1,2,0:T(2,128)(2,1)}), bf16[4,64,2]{1,2,0:T(2,128)(2,1)S(1)}, u32[]{:S(2)}, u32[]{:S(2)}) async-start(bf16[4,64,2]{1,2,0:T(2,128)(2,1)} %copy.51), calls=%async_computation.4 | async-start | bytes 4096 | tf_op jit(solution)/shard_map/all_to_all | solution.py:127
  77.3 0.6 copy-start.8
  82.8 6.9 %all-to-all-start = ((bf16[4,64,2]{1,2,0:T(2,128)(2,1)}), bf16[4,64,2]{1,2,0:T(2,128)(2,1)S(1)}, u32[]{:S(2)}, u32[]{:S(2)}) async-start(bf16[4,64,2]{1,2,0:T(2,128)(2,1)} %copy.49), calls=%async_computation | async-start | bytes 4096 | tf_op jit(solution)/shard_map/all_to_all | solution.py:93
  86.0 265.2 %all-reduce.2.cloned.1.call-start = ((), (), s32[]{:S(2)}) async-start(), calls=%async_computation.7 | async-start | bytes 2097152 | tf_op jit(solution)/shard_map/psum | solution.py:156
  89.2 276.1 %reduce-scatter.5.cloned.1.call-start = ((), (), s32[]{:S(2)}) async-start(), calls=%async_computation.9 | async-start | bytes 7077888 | tf_op jit(solution)/shard_map/reduce_scatter | solution.py:163
  95.7 336.9 %reduce-scatter.3.cloned.1.call-start = ((), (), s32[]{:S(2)}) async-start(), calls=%async_computation.8 | async-start | bytes 14155776 | tf_op jit(solution)/shard_map/reduce_scatter | solution.py:160
  117.8 236.0 %copy-start.10 = (s32[1024]{0:T(1024)S(1)}, s32[1024]{0:T(1024)}, u32[]{:S(2)}) copy-start(s32[1024]{0:T(1024)} %copy-done.9) | copy-start | bytes 12292
  117.8 236.0 %all-to-all-start.3 = ((bf16[4,64,2048]{2,1,0:T(8,128)(2,1)}), bf16[4,64,2048]{2,1,0:T(8,128)(2,1)S(1)}, u32[]{:S(2)}, u32[]{:S(2)}) async-start(bf16[4,64,2048]{2,1,0:T(8,128)(2,1)} %bitcast.9), calls=%async_computation.3 | async-start | bytes 2097152 | tf_op jit(solution)/shard_map/all_to_all | solution.py:120
  356.3 2.3 copy-start.6
  356.3 76.3 %copy-start.1 = (bf16[128,2048]{1,0:T(8,128)(2,1)S(1)}, bf16[128,2048]{1,0:T(8,128)(2,1)}, u32[]{:S(2)}) copy-start(bf16[128,2048]{1,0:T(8,128)(2,1)} %param.7) | copy-start | bytes 1572868
  358.6 5.6 %copy-start.4 = (bf16[2048,128]{1,0:T(8,128)(2,1)S(1)}, bf16[2048,128]{1,0:T(8,128)(2,1)}, u32[]{:S(2)}) copy-start(bf16[2048,128]{1,0:T(8,128)(2,1)} %param.10) | copy-start | bytes 1572868
Sparse Core Ops, SparseCore 0:
  92.6 258.5 all-reduce.1
Sparse Core Ops, SparseCore 1:
  95.8 123.6 reduce-scatter.4
  223.5 209.1 reduce-scatter.2
where the time goes:
time: 441 us; the launch traced here: 440 us
  waiting for transfers between devices  316 us (72%)
  matrix products  43.3 us (10%)
  local copies, waits for them, and re-layouts  26.9 us (6%)
  other arithmetic  19.7 us (4%)
  starting transfers between devices  18.5 us (4%)
  between operations  15.8 us (4%)
    psum x1, waiting for transfers between devices, per_device(): router_grad = lax.psum(router_part, ('dp', 'expert'))  230 us
    reduce_scatter x1, waiting for transfers between devices, per_device(): lax.psum_scatter(part_gateup[None], 'dp', scatter_dimension=1, tiled=True)  67.3 us
    all_to_all x1, waiting for transfers between devices, per_device(): lax.all_to_all(send_in.reshape(flight, capacity, width), 'expert', split_...  13.1 us
    dot_general x1, matrix products, expert_rows(): pre_act = jnp.dot(rows_in, w_gateup, preferred_element_type=jnp.float32)  9.69 us
    dot_general x1, matrix products, expert_rows(): lax.dot_general(pre_grad, w_gateup, (((1,), (1,)), ((), ())), preferred_e...  9.05 us
  transfers between devices with their start and end apart: 8, of which 6 were waited for; matrix products, arithmetic and copies ran while one was open for 13% of the time, Pallas kernels for 0%

commit v1 on v0

--- a/solution.py
+++ b/solution.py
@@ -1,7 +1,15 @@
+import functools
 import jax
 import jax.numpy as jnp
 from jax import lax
 from jax.sharding import PartitionSpec as P
+
+
+def place_the_seats_all(shard_in, mesh_dim):
+    return lax.all_gather(shard_in, mesh_dim).sum(axis=0)
+
+
+pair_series = functools.partial(place_the_seats_all, mesh_dim=("dp", "expert"))
 
 
 def expert_rows(rows_in, rows_grad, w_gateup, w_down, acc_gateup, acc_down):
@@ -153,7 +161,7 @@
     router_part = lax.dot_general(
         tokens, logit_grad, (((0,), (0,)), ((), ())), preferred_element_type=jnp.float32
     )
-    router_grad = lax.psum(router_part, ("dp", "expert"))
+    router_grad = pair_series(router_part)
     part_gateup = acc_gateup.astype(jnp.bfloat16)
     part_down = acc_down.astype(jnp.bfloat16)
     gate_up_grad, down_grad = (

time: 441 us -> 550 us (1.25)
  waiting for transfers between devices: 316 us -> 383 us
  local copies, waits for them, and re-layouts: 26.9 us -> 55.7 us
  blocking collectives: 0 us -> 23 us
  starting transfers between devices: 18.5 us -> 11.3 us
    psum x1 -> x0, waiting for transfers between devices: 230 us -> none  [per_device(): router_grad = lax.psum(router_part, ('dp', 'expert'))]
    all_gather x0 -> x1, waiting for transfers between devices: none -> 166 us  [place_the_seats_all(): return lax.all_gather(shard_in, mesh_dim).sum(axis=0)]
    reduce_scatter x1, waiting for transfers between devices: 67.3 us -> 195 us  [per_device(): lax.psum_scatter(part_gateup[None], 'dp', scatter_dimension=1, tiled=True)]
    unnamed x28 -> x31, local copies, waits for them, and re-layouts: 4.61 us -> 32.6 us
    all_to_all x0 -> x2, blocking collectives: none -> 23 us  [the longest x1 16.9 us: per_device(): lax.all_to_all(back_rows.reshape(sources, capacity, width), 'expert', spl...]
    all_to_all x2 -> x0, starting transfers between devices: 7.09 us -> none  [the longest x1 3.87 us: per_device(): lax.all_to_all(back_rows.reshape(sources, capacity, width), 'expert', spl...]
    reduce_sum x0 -> x1, other arithmetic: none -> 6.8 us  [place_the_seats_all(): return lax.all_gather(shard_in, mesh_dim).sum(axis=0)]
  transfers between devices with their start and end apart: 8 -> 6, of which waited for: 6 -> 5; matrix products, arithmetic and copies ran while one was open for 13% -> 16% of each run, Pallas kernels for 0% -> 0%
where the time goes in v1:
time: 550 us; the launch traced here: 549 us
  waiting for transfers between devices  383 us (70%)
  local copies, waits for them, and re-layouts  55.7 us (10%)
  matrix products  39.1 us (7%)
  blocking collectives  23 us (4%)
  other arithmetic  20.6 us (4%)
  between operations  15.8 us (3%)
  starting transfers between devices  11.3 us (2%)
    reduce_scatter x1, waiting for transfers between devices, per_device(): lax.psum_scatter(part_gateup[None], 'dp', scatter_dimension=1, tiled=True)  195 us
    all_gather x1, waiting for transfers between devices, place_the_seats_all(): return lax.all_gather(shard_in, mesh_dim).sum(axis=0)  166 us
    unnamed x31, local copies, waits for them, and re-layouts  32.6 us
    all_to_all x1, blocking collectives, per_device(): lax.all_to_all(back_rows.reshape(sources, capacity, width), 'expert', spl...  16.9 us
    all_to_all x1, waiting for transfers between devices, per_device(): lax.all_to_all(send_in.reshape(flight, capacity, width), 'expert', split_...  13.1 us
  transfers between devices with their start and end apart: 6, of which 5 were waited for; matrix products, arithmetic and copies ran while one was open for 16% of the time, Pallas kernels for 0%

profile of v1, /device:TPU:0, one launch (start us, length us, event | category | flops | bytes accessed | tf_op | source)
XLA Modules:
  0.0 548.9 jit_solution(1274616684275924743)
XLA Ops:
  13.3 2.4 scatter_custom_fusion.1
  15.8 2.4 scatter_custom_fusion
  23.2 4.4 all-to-all-start.2
  28.9 13.1 %all-to-all-done.2 = bf16[4,64,2048]{2,1,0:T(8,128)(2,1)S(1)} async-done(((bf16[4,64,2048]{2,1,0:T(8,128)(2,1)}), bf16[4,64,2048]{2,1,0:T(8,128)(2,1)S(1)}, u32[]{:S(2)}, u32[]{:S(2)}) %all-to-all-start.2) | async-done | bytes 1048608 | tf_op jit(solution)/shard_map/all_to_all | solution.py:87
  42.0 3.5 all-to-all-start.1
  45.6 6.4 %fusion.2 = f32[256,3072]{1,0:T(8,128)S(1)} fusion(bf16[256,2048]{1,0:T(8,128)(2,1)S(1)} %bitcast.87, bf16[1,2048,3072]{2,1,0:T(8,128)(2,1)} %param.12), kind=kOutput, calls=%fused_computation.10 | convolution fusion | flops 3221225472 | bytes 16777216 | tf_op jit(solution)/shard_map/dot_general | solution.py:17
  54.1 5.9 %all-to-all-done.1 = bf16[4,64,2048]{2,1,0:T(8,128)(2,1)S(1)} async-done(((bf16[4,64,2048]{2,1,0:T(8,128)(2,1)}), bf16[4,64,2048]{2,1,0:T(8,128)(2,1)S(1)}, u32[]{:S(2)}, u32[]{:S(2)}) %all-to-all-start.1) | async-done | bytes 1048608 | tf_op jit(solution)/shard_map/all_to_all | solution.py:94
  59.9 4.7 fusion.24
  65.3 3.2 all-to-all-start.4
  69.1 3.1 all-to-all-done.4
  72.3 3.5 gather_fusion.4
  82.4 6.1 %all_to_all.25 = bf16[4,64,2]{1,2,0:T(2,128)(2,1)S(1)} all-to-all(bf16[4,64,2]{1,2,0:T(2,128)(2,1)S(1)} %copy.47), channel_id=1, replica_groups=mesh['dp'=8,'expert'=4] {'expert'}, dimensions={0} | all-to-all | bytes 2048 | tf_op jit(solution)/shard_map/all_to_all | solution.py:101
  90.0 4.5 fusion.4
  94.9 6.0 %multiply_convert_fusion.3 = (bf16[256,1536]{1,0:T(8,128)(2,1)S(1)}, bf16[256,1536]{1,0:T(8,128)(2,1)S(1)}) fusion(f32[256,3072]{1,0:T(8,128)} %copy-done.3, bf16[256,2048]{1,0:T(8,128)(2,1)S(1)} %bitcast.91, bf16[1,1536,2048]{2,1,0:T(8,128)(2,1)} %param.13), kind=kOutput, calls=%fused_computation.33 | convolution fusion | flops 1615724544 | bytes 12058624 | tf_op jit(solution)/shard_map/dot_general | solution.py:23
  100.9 6.7 %convert_bitcast_fusion = bf16[1,2048,3072]{2,1,0:T(8,128)(2,1)} fusion(bf16[256,2048]{1,0:T(8,128)(2,1)S(1)} %bitcast.88, bf16[256,1536]{1,0:T(8,128)(2,1)S(1)} %get-tuple-element.23, bf16[256,1536]{1,0:T(8,128)(2,1)S(1)} %get-tuple-element.22), kind=kOutput, calls=%fused_computation.12 | convolution fusion | flops 3230662656 | bytes 15204352 | tf_op jit(solution)/shard_map/dot_general | solution.py:33
  107.7 8.1 %fusion.18 = bf16[256,2048]{1,0:T(8,128)(2,1)S(1)} fusion(bf16[1,2048,3072]{2,1,0:T(8,128)(2,1)} %param.12, bf16[256,1536]{1,0:T(8,128)(2,1)S(1)} %get-tuple-element.23, bf16[256,1536]{1,0:T(8,128)(2,1)S(1)} %get-tuple-element.22), kind=kOutput, calls=%fused_computation.23 | convolution fusion | flops 3224895488 | bytes 15204352 | tf_op jit(solution)/shard_map/dot_general | solution.py:36
  115.8 16.9 %all_to_all.26 = bf16[4,64,2048]{2,1,0:T(8,128)(2,1)S(1)} all-to-all(bf16[4,64,2048]{2,1,0:T(8,128)(2,1)S(1)} %bitcast.92), channel_id=1, replica_groups=mesh['dp'=8,'expert'=4] {'expert'}, dimensions={0} | all-to-all | bytes 2097152 | tf_op jit(solution)/shard_map/all_to_all | solution.py:128
  132.6 3.3 gather_fusion.3
  136.0 2.7 gather.29
  138.7 3.9 convert_reduce_fusion
  143.8 166.0 %all-gather.3.cloned.1.call-done = f32[65536,128]{0,1:T(8,128)} async-done(((f32[2048,128]{0,1:T(8,128)}), f32[65536,128]{0,1:T(8,128)}) %all-gather.3.cloned.1.call-update) | async-done | bytes 33554448 | tf_op jit(solution)/shard_map/all_gather | solution.py:9
  309.8 28.2 %copy.55 = f32[16,8,32,2048]{3,2,1,0:T(8,128)S(1)} copy(f32[16,8,32,2048]{3,1,2,0:T(8,128)} %bitcast.85) | data formatting | bytes 67108864
  338.0 6.8 %bitcast_reduce_fusion = f32[2048,128]{0,1:T(8,128)S(1)} fusion(f32[16,8,32,2048]{3,2,1,0:T(8,128)S(1)} %copy.55), kind=kLoop, calls=%fused_computation.7 | loop fusion | flops 8126464 | bytes 34603008 | tf_op jit(solution)/shard_map/reduce_sum | solution.py:9
  346.2 195.3 %reduce-scatter.3.cloned.1.call-done = bf16[1,256,3072]{2,1,0:T(8,128)(2,1)} async-done(((bf16[1,2048,3072]{2,1,0:T(8,128)(2,1)}), bf16[1,256,3072]{2,1,0:T(8,128)(2,1)}) %reduce-scatter.3.cloned.1.call-update) | async-done | bytes 1572880 | tf_op jit(solution)/shard_map/reduce_scatter | solution.py:168
  (99 shorter events, 25.8 us)
Async XLA Ops:
  8.0 10.9 %copy-start = (bf16[128,2048]{1,0:T(8,128)(2,1)S(1)}, bf16[128,2048]{1,0:T(8,128)(2,1)}, u32[]{:S(2)}) copy-start(bf16[128,2048]{1,0:T(8,128)(2,1)} %param.7) | copy-start | bytes 1572868
  10.6 0.6 copy-start.6
  18.2 0.7 copy-start.11
  18.9 1.4 copy-start.2
  23.2 4.4 copy-start.4
  23.2 4.9 copy-start.8
  23.2 5.1 copy-start.13
  23.2 18.8 %all-to-all-start.2 = ((bf16[4,64,2048]{2,1,0:T(8,128)(2,1)}), bf16[4,64,2048]{2,1,0:T(8,128)(2,1)S(1)}, u32[]{:S(2)}, u32[]{:S(2)}) async-start(bf16[4,64,2048]{2,1,0:T(8,128)(2,1)} %get-tuple-element.30), calls=%async_computation.2 | async-start | bytes 2097152 | tf_op jit(solution)/shard_map/all_to_all | solution.py:87
  28.1 44.2 %copy-start.9 = (s32[1024]{0:T(1024)}, s32[1024]{0:T(1024)S(1)}, u32[]{:S(2)}) copy-start(s32[1024]{0:T(1024)S(1)} %pad_clamp_fusion) | copy-start | bytes 12292
  42.0 17.9 %all-to-all-start.1 = ((bf16[4,64,2048]{2,1,0:T(8,128)(2,1)}), bf16[4,64,2048]{2,1,0:T(8,128)(2,1)S(1)}, u32[]{:S(2)}, u32[]{:S(2)}) async-start(bf16[4,64,2048]{2,1,0:T(8,128)(2,1)} %get-tuple-element.31), calls=%async_computation.1 | async-start | bytes 2097152 | tf_op jit(solution)/shard_map/all_to_all | solution.py:94
  52.0 1.6 copy-start.3
  65.3 6.9 %all-to-all-start.4 = ((bf16[4,64,2]{1,2,0:T(2,128)(2,1)}), bf16[4,64,2]{1,2,0:T(2,128)(2,1)S(1)}, u32[]{:S(2)}, u32[]{:S(2)}) async-start(bf16[4,64,2]{1,2,0:T(2,128)(2,1)} %copy.49), calls=%async_computation.4 | async-start | bytes 4096 | tf_op jit(solution)/shard_map/all_to_all | solution.py:135
  68.5 241.3 %all-gather.3.cloned.1.call-start = ((), (), s32[]{:S(2)}) async-start(), calls=%async_computation.9 | async-start | bytes 34603008 | tf_op jit(solution)/shard_map/all_gather | solution.py:9
  76.9 5.3 copy-start.12
  79.8 266.4 %reduce-scatter.5.cloned.1.call-start = ((), (), s32[]{:S(2)}) async-start(), calls=%async_computation.8 | async-start | bytes 7077888 | tf_op jit(solution)/shard_map/reduce_scatter | solution.py:171
  94.5 447.0 %reduce-scatter.3.cloned.1.call-start = ((), (), s32[]{:S(2)}) async-start(), calls=%async_computation.7 | async-start | bytes 14155776 | tf_op jit(solution)/shard_map/reduce_scatter | solution.py:168
  115.8 16.9 %copy-start.10 = (s32[1024]{0:T(1024)S(1)}, s32[1024]{0:T(1024)}, u32[]{:S(2)}) copy-start(s32[1024]{0:T(1024)} %copy-done.9) | copy-start | bytes 12292
  135.9 2.8 copy-start.7
  138.7 3.9 copy-start.5
  338.0 203.4 %copy-start.1 = (bf16[128,2048]{1,0:T(8,128)(2,1)S(1)}, bf16[128,2048]{1,0:T(8,128)(2,1)}, u32[]{:S(2)}) copy-start(bf16[128,2048]{1,0:T(8,128)(2,1)} %param.7) | copy-start | bytes 1572868
Sparse Core Ops, SparseCore 0:
  79.9 229.8 all-gather.2
Sparse Core Ops, SparseCore 1:
  94.6 236.5 reduce-scatter.4
  335.2 206.2 reduce-scatter.2
